TPU v7x, 128 devices: a whole 4x4x4 slice. The times are simulated.
128 devices in a mesh: section: 4 (over x_lo, core), tok: 32 (over y, z, x_hi).
Axes of the slice: x: 4 (x_hi: 2, x_lo: 2; x = x_hi * 2 + x_lo), y: 4, z: 4, core: 2. Of those that a mesh axis runs over, the one named last changes fastest.
Arguments:
- states: bfloat16 [8, 2048, 4096], P('section', 'tok'), may hold values from -60 to 60
- spans: int32 [2, 2], replicated, may hold values from 0 to 7, as said below
Outputs:
- bridges: float32 [2, 4096, 4096], P(None, 'section', 'tok')
- residuals: float32 [2, 4096, 4096], P(None, 'section', 'tok')
Inputs may be any that keep to these rules, and one draw needn't show every extreme that they name: `spans`: each row is (start, end) with end - start at least 2.
All inputs are finite; a program needn't handle non-finite values.
Results may differ from a plain program's by a relative error of at most 0.0093.
Values may be sent and summed in bfloat16 or wider, within the bound.
A program may use at most 64 MiB of HBM per device.

v0:
```python
import jax
import jax.numpy as jnp
from jax import lax
from jax.sharding import Mesh
from jax.sharding import PartitionSpec as P

CG_STEPS = 2
SECTION = ("section_0", "section_1")
TOK = ("tok_0", "tok_1", "tok_2")
SECTION_TOK = ("section_0", "section_1", "tok_0", "tok_1", "tok_2")
RIDGE = 0.25


def padded_to(lines, devices):
    spare = -lines.shape[0] % devices
    if not spare:
        return lines
    return jnp.concatenate([lines, jnp.zeros((spare, *lines.shape[1:]), lines.dtype)])


def from_root(value, axis, root):
    lines = jnp.where(lax.axis_index(axis) == root, value, jnp.zeros_like(value)).reshape(
        -1, *value.shape[1:][-1:]
    )
    padded = padded_to(lines, lax.axis_size(axis))
    own = lax.psum_scatter(padded, axis, scatter_dimension=0, tiled=True)
    return lax.all_gather(own, axis, axis=0, tiled=True)[: len(lines)].reshape(value.shape)


def in_blocks(value, dim, devices):
    before, after = (value.shape[:dim], value.shape[dim + 1 :])
    return jnp.moveaxis(value.reshape(*before, devices, -1, *after), dim, 0)


def sum_at_owner(value, axis, dim):
    devices = lax.axis_size(axis)
    blocks = lax.all_to_all(in_blocks(value, dim, devices), axis, 0, 0, tiled=True)
    return jnp.sum(blocks, axis=0)


def joined_along(blocks, dim):
    blocks = jnp.moveaxis(blocks, 0, dim)
    lengths = blocks.shape
    return blocks.reshape(*lengths[:dim], lengths[dim] * lengths[dim + 1], *lengths[dim + 2 :])


def copy_for_each(value, axis):
    copies = jnp.broadcast_to(value, (lax.axis_size(axis), *value.shape))
    return lax.all_to_all(copies, axis, split_axis=0, concat_axis=0, tiled=True)


def gather_directly(value, axis, dim):
    return joined_along(copy_for_each(value, axis), dim)


def over_axes(value, axes):
    for axis in axes:
        value = lax.psum(value, axis)
    return value


def transposed(left, right_hand):
    return lax.dot_general(
        left, right_hand, (((0,), (0,)), ((), ())), preferred_element_type=jnp.float32
    )


def conjugate(operators, rights, summed):
    bridges = [jnp.zeros_like(right_side) for right_side in rights]
    residuals = list(rights)
    directions = list(rights)
    squares = summed([jnp.sum(right_side * right_side) for right_side in rights])
    for step in range(CG_STEPS):
        images = [operators[k](directions[k]) for k in range(len(rights))]
        curvatures = summed([jnp.sum(directions[k] * images[k]) for k in range(len(rights))])
        for k in range(len(rights)):
            step_size = squares[k] / curvatures[k]
            bridges[k] = bridges[k] + step_size * directions[k]
            residuals[k] = residuals[k] - step_size * images[k]
        if step + 1 < CG_STEPS:
            renewed = summed([jnp.sum(residual * residual) for residual in residuals])
            for k in range(len(rights)):
                directions[k] = residuals[k] + renewed[k] / squares[k] * directions[k]
            squares = renewed
    return (bridges, residuals)


def per_device(states, spans):
    sections = lax.axis_size(SECTION)
    section_index = lax.axis_index(SECTION)
    tok_count = lax.axis_size(TOK)
    layers_here, tok_rows, feature_width = states.shape
    total_rows = tok_rows * tok_count
    scaling = 1.0 / total_rows
    block_width = feature_width // sections

    def fetch(boundary):
        picked = lax.dynamic_index_in_dim(states, boundary % layers_here, 0, keepdims=False)
        return from_root(picked, SECTION, boundary // layers_here)

    def prepare(k):
        source = fetch(spans[k, 0])
        target = fetch(spans[k, 1])
        target_cols = lax.all_to_all(target, TOK, split_axis=1, concat_axis=0, tiled=True)
        sliced = lax.dynamic_slice_in_dim(source, section_index * block_width, block_width, 1)
        source_cols = lax.all_gather(sliced, TOK, axis=0, tiled=True)
        right_side = transposed(source_cols, target_cols) * scaling

        def operator(direction):
            direction_low = direction.astype(jnp.bfloat16)
            shared = sum_at_owner(
                jnp.dot(source_cols, direction_low, preferred_element_type=jnp.float32), SECTION, 0
            )
            mapped = gather_directly(shared.astype(jnp.bfloat16), SECTION, 0)
            return transposed(source_cols, mapped) * scaling + RIDGE * direction

        return (operator, right_side)

    setups = [prepare(k) for k in range(spans.shape[0])]

    def summed(values):
        totals = over_axes(jnp.stack(values), SECTION_TOK)
        return [totals[k] for k in range(len(values))]

    bridges, residuals = conjugate(
        [entry[0] for entry in setups], [entry[1] for entry in setups], summed
    )
    return (jnp.stack(bridges), jnp.stack(residuals))


def solution(mesh):
    split = Mesh(
        mesh.devices.reshape(2, 2, 4, 4, 2), ("section_0", "section_1", "tok_0", "tok_1", "tok_2")
    )
    return jax.shard_map(
        per_device,
        mesh=split,
        in_specs=(P(SECTION, TOK, None), P()),
        out_specs=(P(None, SECTION, TOK), P(None, SECTION, TOK)),
        check_vma=False,
    )
```

profile of v0, /device:TPU:0, one launch (start us, length us, event | category | flops | bytes accessed | tf_op | source)
XLA Modules:
  0.0 532.0 jit_solution(17612834347519697008)
XLA Ops:
  24.2 18.6 %reduce-scatter.5.cloned.1.call-done = bf16[16,4096]{1,0:T(8,128)(2,1)} async-done(((bf16[64,4096]{1,0:T(8,128)(2,1)}), bf16[16,4096]{1,0:T(8,128)(2,1)}) %reduce-scatter.5.cloned.1.call-update) | async-done | bytes 131088 | tf_op jit(solution)/shard_map/reduce_scatter | solution.py:26
  42.7 7.8 %all_gather.18 = bf16[64,4096]{1,0:T(8,128)(2,1)S(1)} all-gather(bf16[16,4096]{1,0:T(8,128)(2,1)} %reduce-scatter.5.cloned.1.call-done), channel_id=1, replica_groups=mesh['section_0'=2,'section_1'=2,'tok_0'=4,'tok_1'=4,'tok_2'=2] {'sectio..., dimensions={0}, use_global_device_ids=true | all-gather | bytes 655360 | tf_op jit(solution)/shard_map/all_gather | solution.py:27
  51.3 13.2 %reduce-scatter.9.cloned.1.call-done = bf16[16,4096]{1,0:T(8,128)(2,1)} async-done(((bf16[64,4096]{1,0:T(8,128)(2,1)}), bf16[16,4096]{1,0:T(8,128)(2,1)}) %reduce-scatter.9.cloned.1.call-update) | async-done | bytes 131088 | tf_op jit(solution)/shard_map/reduce_scatter | solution.py:26
  64.5 7.8 %all_gather.21 = bf16[64,4096]{1,0:T(8,128)(2,1)S(1)} all-gather(bf16[16,4096]{1,0:T(8,128)(2,1)} %reduce-scatter.9.cloned.1.call-done), channel_id=1, replica_groups=mesh['section_0'=2,'section_1'=2,'tok_0'=4,'tok_1'=4,'tok_2'=2] {'sectio..., dimensions={0}, use_global_device_ids=true | all-gather | bytes 655360 | tf_op jit(solution)/shard_map/all_gather | solution.py:27
  73.0 13.8 %reduce-scatter.7.cloned.1.call-done = bf16[16,4096]{1,0:T(8,128)(2,1)} async-done(((bf16[64,4096]{1,0:T(8,128)(2,1)}), bf16[16,4096]{1,0:T(8,128)(2,1)}) %reduce-scatter.7.cloned.1.call-update) | async-done | bytes 131088 | tf_op jit(solution)/shard_map/reduce_scatter | solution.py:26
  86.8 7.8 %all_gather.20 = bf16[64,4096]{1,0:T(8,128)(2,1)S(1)} all-gather(bf16[16,4096]{1,0:T(8,128)(2,1)} %reduce-scatter.7.cloned.1.call-done), channel_id=1, replica_groups=mesh['section_0'=2,'section_1'=2,'tok_0'=4,'tok_1'=4,'tok_2'=2] {'sectio..., dimensions={0}, use_global_device_ids=true | all-gather | bytes 655360 | tf_op jit(solution)/shard_map/all_gather | solution.py:27
  95.6 9.4 %all-to-all-start = ((bf16[64,32,128]{2,0,1:T(8,128)(2,1)}), bf16[64,32,128]{2,0,1:T(8,128)(2,1)S(1)}, u32[]{:S(2)}, u32[]{:S(2)}) async-start(bf16[64,32,128]{2,0,1:T(8,128)(2,1)} %copy_bitcast_fusion.1), calls=%async_computation.2 | async-start | bytes 1048576 | tf_op jit(solution)/shard_map/all_to_all | solution.py:104
  105.0 4.7 reduce-scatter.11.cloned.1.call-done
  109.7 7.4 %all_gather.23 = bf16[64,4096]{1,0:T(8,128)(2,1)S(1)} all-gather(bf16[16,4096]{1,0:T(8,128)(2,1)} %reduce-scatter.11.cloned.1.call-done), channel_id=1, replica_groups=mesh['section_0'=2,'section_1'=2,'tok_0'=4,'tok_1'=4,'tok_2'=2] {'sectio..., dimensions={0}, use_global_device_ids=true | all-gather | bytes 655360 | tf_op jit(solution)/shard_map/all_gather | solution.py:27
  120.2 7.3 %all-to-all-start.1 = ((bf16[64,32,128]{2,0,1:T(8,128)(2,1)}), bf16[64,32,128]{2,0,1:T(8,128)(2,1)S(1)}, u32[]{:S(2)}, u32[]{:S(2)}) async-start(bf16[64,32,128]{2,0,1:T(8,128)(2,1)} %copy_bitcast_fusion), calls=%async_computation.5 | async-start | bytes 1048576 | tf_op jit(solution)/shard_map/all_to_all | solution.py:104
  127.5 68.5 %all-gather.3.cloned.1.call-done = bf16[2048,1024]{1,0:T(8,128)(2,1)} async-done(((bf16[64,1024]{1,0:T(8,128)(2,1)}), bf16[2048,1024]{1,0:T(8,128)(2,1)}) %all-gather.3.cloned.1.call-update) | async-done | bytes 4194320 | tf_op jit(solution)/shard_map/all_gather | solution.py:106
  205.4 73.2 %all-gather.5.cloned.1.call-done = bf16[2048,1024]{1,0:T(8,128)(2,1)} async-done(((bf16[64,1024]{1,0:T(8,128)(2,1)}), bf16[2048,1024]{1,0:T(8,128)(2,1)}) %all-gather.5.cloned.1.call-update) | async-done | bytes 4194320 | tf_op jit(solution)/shard_map/all_gather | solution.py:106
  288.1 14.3 %all-to-all-done.4 = f32[4,512,128]{2,1,0:T(8,128)S(1)} async-done(((f32[4,512,128]{2,1,0:T(8,128)}), f32[4,512,128]{2,1,0:T(8,128)S(1)}, u32[]{:S(2)}, u32[]{:S(2)}) %all-to-all-start.4) | async-done | bytes 1048608 | tf_op jit(solution)/shard_map/all_to_all | solution.py:37
  306.8 8.7 %all-to-all-done.3 = bf16[4,512,128]{2,1,0:T(8,128)(2,1)S(1)} async-done(((bf16[4,512,128]{2,1,0:T(8,128)(2,1)}), bf16[4,512,128]{2,1,0:T(8,128)(2,1)S(1)}, u32[]{:S(2)}, u32[]{:S(2)}) %all-to-all-start.3) | async-done | bytes 524320 | tf_op jit(solution)/shard_map/all_to_all | solution.py:49
  324.3 4.6 all-to-all-done.5
  335.5 4.9 all-reduce.4
  342.8 10.1 %all-reduce.1 = (f32[2]{0:T(128)S(1)}, f32[2]{0:T(128)S(1)}) all-reduce(f32[2]{0:T(128)S(1)} %get-tuple-element.12, f32[2]{0:T(128)S(1)} %get-tuple-element.13), channel_id=1, replica_groups=mesh['section_0'=2,'section_1'=2,'tok_0'=4,'tok_1'=4,'tok_2'=2] {'tok_0'}, use_global_device_ids=true, to_apply=%region_8.9 | all-reduce | flops 4 | bytes 32 | tf_op jit(solution)/shard_map/psum | solution.py:58
  352.9 10.7 %all-reduce = (f32[2]{0:T(128)S(1)}, f32[2]{0:T(128)S(1)}) all-reduce(f32[2]{0:T(128)S(1)} %get-tuple-element.8, f32[2]{0:T(128)S(1)} %get-tuple-element.9), channel_id=1, replica_groups=mesh['section_0'=2,'section_1'=2,'tok_0'=4,'tok_1'=4,'tok_2'=2] {'tok_1'}, use_global_device_ids=true, to_apply=%region_9.10 | all-reduce | flops 4 | bytes 32 | tf_op jit(solution)/shard_map/psum | solution.py:58
  363.6 6.6 %all-reduce.2 = (f32[2]{0:T(128)S(1)}, f32[2]{0:T(128)S(1)}) all-reduce(f32[2]{0:T(128)S(1)} %get-tuple-element.6, f32[2]{0:T(128)S(1)} %get-tuple-element.7), channel_id=1, replica_groups=mesh['section_0'=2,'section_1'=2,'tok_0'=4,'tok_1'=4,'tok_2'=2] {'tok_2'}, use_global_device_ids=true, to_apply=%region_10.11 | all-reduce | flops 4 | bytes 32 | tf_op jit(solution)/shard_map/psum | solution.py:58
  377.1 4.9 psum.150
  384.4 7.7 %psum.152 = f32[2]{0:T(128)S(1)} all-reduce(f32[2]{0:T(128)S(1)} %psum.151), channel_id=1, replica_groups=mesh['section_0'=2,'section_1'=2,'tok_0'=4,'tok_1'=4,'tok_2'=2] {'tok_0'}, use_global_device_ids=true, to_apply=%region_24.25 | all-reduce | flops 2 | bytes 16 | tf_op jit(solution)/shard_map/psum | solution.py:58
  392.1 7.7 %psum.153 = f32[2]{0:T(128)S(1)} all-reduce(f32[2]{0:T(128)S(1)} %psum.152), channel_id=1, replica_groups=mesh['section_0'=2,'section_1'=2,'tok_0'=4,'tok_1'=4,'tok_2'=2] {'tok_1'}, use_global_device_ids=true, to_apply=%region_25.26 | all-reduce | flops 2 | bytes 16 | tf_op jit(solution)/shard_map/psum | solution.py:58
  399.8 6.4 %psum.154 = f32[2]{0:T(128)S(1)} all-reduce(f32[2]{0:T(128)S(1)} %psum.153), channel_id=1, replica_groups=mesh['section_0'=2,'section_1'=2,'tok_0'=4,'tok_1'=4,'tok_2'=2] {'tok_2'}, use_global_device_ids=true, to_apply=%region_26.27 | all-reduce | flops 2 | bytes 16 | tf_op jit(solution)/shard_map/psum | solution.py:58
  422.8 8.6 %all-to-all-done.6 = f32[4,512,128]{2,1,0:T(8,128)} async-done(((f32[4,512,128]{2,1,0:T(8,128)}), f32[4,512,128]{2,1,0:T(8,128)}, u32[]{:S(2)}, u32[]{:S(2)}) %all-to-all-start.6) | async-done | bytes 1048608 | tf_op jit(solution)/shard_map/all_to_all | solution.py:37
  437.0 13.2 %all-to-all-done.8 = f32[4,512,128]{2,1,0:T(8,128)} async-done(((f32[4,512,128]{2,1,0:T(8,128)}), f32[4,512,128]{2,1,0:T(8,128)}, u32[]{:S(2)}, u32[]{:S(2)}) %all-to-all-start.8) | async-done | bytes 1048608 | tf_op jit(solution)/shard_map/all_to_all | solution.py:37
  456.5 7.6 %all-to-all-done.7 = bf16[4,512,128]{2,1,0:T(8,128)(2,1)} async-done(((bf16[4,512,128]{2,1,0:T(8,128)(2,1)}), bf16[4,512,128]{2,1,0:T(8,128)(2,1)}, u32[]{:S(2)}, u32[]{:S(2)}) %all-to-all-start.7) | async-done | bytes 524320 | tf_op jit(solution)/shard_map/all_to_all | solution.py:49
  469.1 5.0 multiply_reduce_fusion.1
  478.0 5.0 multiply_reduce_fusion
  484.3 4.9 psum.155
  491.7 9.7 %psum.157 = f32[2]{0:T(128)S(1)} all-reduce(f32[2]{0:T(128)S(1)} %psum.156), channel_id=1, replica_groups=mesh['section_0'=2,'section_1'=2,'tok_0'=4,'tok_1'=4,'tok_2'=2] {'tok_0'}, use_global_device_ids=true, to_apply=%region_33.34 | all-reduce | flops 2 | bytes 16 | tf_op jit(solution)/shard_map/psum | solution.py:58
  501.4 9.7 %psum.158 = f32[2]{0:T(128)S(1)} all-reduce(f32[2]{0:T(128)S(1)} %psum.157), channel_id=1, replica_groups=mesh['section_0'=2,'section_1'=2,'tok_0'=4,'tok_1'=4,'tok_2'=2] {'tok_1'}, use_global_device_ids=true, to_apply=%region_34.35 | all-reduce | flops 2 | bytes 16 | tf_op jit(solution)/shard_map/psum | solution.py:58
  511.1 6.4 %psum.159 = f32[2]{0:T(128)S(1)} all-reduce(f32[2]{0:T(128)S(1)} %psum.158), channel_id=1, replica_groups=mesh['section_0'=2,'section_1'=2,'tok_0'=4,'tok_1'=4,'tok_2'=2] {'tok_2'}, use_global_device_ids=true, to_apply=%region_35.36 | all-reduce | flops 2 | bytes 16 | tf_op jit(solution)/shard_map/psum | solution.py:58
  (70 shorter events, 103.1 us)
Async XLA Ops:
  7.2 35.6 %reduce-scatter.5.cloned.1.call-start = ((), (), s32[]{:S(2)}) async-start(), calls=%async_computation.14 | async-start | bytes 655360 | tf_op jit(solution)/shard_map/reduce_scatter | solution.py:26
  22.1 42.4 %reduce-scatter.9.cloned.1.call-start = ((), (), s32[]{:S(2)}) async-start(), calls=%async_computation.17 | async-start | bytes 655360 | tf_op jit(solution)/shard_map/reduce_scatter | solution.py:26
  22.8 64.0 %reduce-scatter.7.cloned.1.call-start = ((), (), s32[]{:S(2)}) async-start(), calls=%async_computation.16 | async-start | bytes 655360 | tf_op jit(solution)/shard_map/reduce_scatter | solution.py:26
  23.5 86.1 %reduce-scatter.11.cloned.1.call-start = ((), (), s32[]{:S(2)}) async-start(), calls=%async_computation.19 | async-start | bytes 655360 | tf_op jit(solution)/shard_map/reduce_scatter | solution.py:26
  24.1 171.9 %all-gather.3.cloned.1.call-start = ((), (), s32[]{:S(2)}) async-start(), calls=%async_computation.15 | async-start | bytes 4325376 | tf_op jit(solution)/shard_map/all_gather | solution.py:106
  51.3 227.4 %all-gather.5.cloned.1.call-start = ((), (), s32[]{:S(2)}) async-start(), calls=%async_computation.18 | async-start | bytes 4325376 | tf_op jit(solution)/shard_map/all_gather | solution.py:106
  95.6 24.6 %all-to-all-start = ((bf16[64,32,128]{2,0,1:T(8,128)(2,1)}), bf16[64,32,128]{2,0,1:T(8,128)(2,1)S(1)}, u32[]{:S(2)}, u32[]{:S(2)}) async-start(bf16[64,32,128]{2,0,1:T(8,128)(2,1)} %copy_bitcast_fusion.1), calls=%async_computation.2 | async-start | bytes 1048576 | tf_op jit(solution)/shard_map/all_to_all | solution.py:104
  120.2 81.7 %all-to-all-start.1 = ((bf16[64,32,128]{2,0,1:T(8,128)(2,1)}), bf16[64,32,128]{2,0,1:T(8,128)(2,1)S(1)}, u32[]{:S(2)}, u32[]{:S(2)}) async-start(bf16[64,32,128]{2,0,1:T(8,128)(2,1)} %copy_bitcast_fusion), calls=%async_computation.5 | async-start | bytes 1048576 | tf_op jit(solution)/shard_map/all_to_all | solution.py:104
  196.0 3.6 copy-start
  201.9 82.6 %all-to-all-start.2 = ((f32[4,512,128]{2,1,0:T(8,128)}), f32[4,512,128]{2,1,0:T(8,128)S(1)}, u32[]{:S(2)}, u32[]{:S(2)}) async-start(f32[4,512,128]{2,1,0:T(8,128)} %bitcast.14), calls=%async_computation.6 | async-start | bytes 2097152 | tf_op jit(solution)/shard_map/all_to_all | solution.py:37
  278.6 3.6 copy-start.1
  284.5 17.9 %all-to-all-start.4 = ((f32[4,512,128]{2,1,0:T(8,128)}), f32[4,512,128]{2,1,0:T(8,128)S(1)}, u32[]{:S(2)}, u32[]{:S(2)}) async-start(f32[4,512,128]{2,1,0:T(8,128)} %bitcast.17), calls=%async_computation.8 | async-start | bytes 2097152 | tf_op jit(solution)/shard_map/all_to_all | solution.py:37
  303.3 12.3 %all-to-all-start.3 = ((bf16[4,512,128]{2,1,0:T(8,128)(2,1)}), bf16[4,512,128]{2,1,0:T(8,128)(2,1)S(1)}, u32[]{:S(2)}, u32[]{:S(2)}) async-start(bf16[4,512,128]{2,1,0:T(8,128)(2,1)} %broadcast_in_dim.12), calls=%async_computation.7 | async-start | bytes 1048576 | tf_op jit(solution)/shard_map/all_to_all | solution.py:49
  315.5 4.5 copy-start.2
  316.6 12.3 %all-to-all-start.5 = ((bf16[4,512,128]{2,1,0:T(8,128)(2,1)}), bf16[4,512,128]{2,1,0:T(8,128)(2,1)S(1)}, u32[]{:S(2)}, u32[]{:S(2)}) async-start(bf16[4,512,128]{2,1,0:T(8,128)(2,1)} %broadcast_in_dim.13), calls=%async_computation.9 | async-start | bytes 1048576 | tf_op jit(solution)/shard_map/all_to_all | solution.py:49
  412.7 18.8 %all-to-all-start.6 = ((f32[4,512,128]{2,1,0:T(8,128)}), f32[4,512,128]{2,1,0:T(8,128)}, u32[]{:S(2)}, u32[]{:S(2)}) async-start(f32[4,512,128]{2,1,0:T(8,128)} %bitcast.25), calls=%async_computation.10 | async-start | bytes 2097152 | tf_op jit(solution)/shard_map/all_to_all | solution.py:37
  431.5 18.8 %all-to-all-start.8 = ((f32[4,512,128]{2,1,0:T(8,128)}), f32[4,512,128]{2,1,0:T(8,128)}, u32[]{:S(2)}, u32[]{:S(2)}) async-start(f32[4,512,128]{2,1,0:T(8,128)} %bitcast.29), calls=%async_computation.12 | async-start | bytes 2097152 | tf_op jit(solution)/shard_map/all_to_all | solution.py:37
  451.1 13.0 %all-to-all-start.7 = ((bf16[4,512,128]{2,1,0:T(8,128)(2,1)}), bf16[4,512,128]{2,1,0:T(8,128)(2,1)}, u32[]{:S(2)}, u32[]{:S(2)}) async-start(bf16[4,512,128]{2,1,0:T(8,128)(2,1)} %broadcast_in_dim.14), calls=%async_computation.11 | async-start | bytes 1048576 | tf_op jit(solution)/shard_map/all_to_all | solution.py:49
  465.0 13.0 %all-to-all-start.9 = ((bf16[4,512,128]{2,1,0:T(8,128)(2,1)}), bf16[4,512,128]{2,1,0:T(8,128)(2,1)}, u32[]{:S(2)}, u32[]{:S(2)}) async-start(bf16[4,512,128]{2,1,0:T(8,128)(2,1)} %broadcast_in_dim.15), calls=%async_computation.13 | async-start | bytes 1048576 | tf_op jit(solution)/shard_map/all_to_all | solution.py:49
Sparse Core Ops, SparseCore 0:
  22.2 20.5 reduce-scatter.4
  45.1 19.3 reduce-scatter.8
  67.5 19.3 reduce-scatter.6
  89.1 20.5 reduce-scatter.10
  112.6 83.3 all-gather.2
  198.9 79.6 all-gather.4
where the time goes:
time: 534 us; the launch traced here: 532 us
  waiting for transfers between devices  257 us (48%)
  blocking collectives  128 us (24%)
  starting transfers between devices  47.7 us (9%)
  matrix products  38.9 us (7%)
  between operations  32.5 us (6%)
  other arithmetic  17.1 us (3%)
  local copies, waits for them, and re-layouts  10.8 us (2%)
    all_gather x2, waiting for transfers between devices, prepare(): source_cols = lax.all_gather(sliced, TOK, axis=0, tiled=True)  142 us
    psum x15, blocking collectives, over_axes(): value = lax.psum(value, axis)  97.1 us
    reduce_scatter x4, waiting for transfers between devices, from_root(): own = lax.psum_scatter(padded, axis, scatter_dimension=0, tiled=True)  50.3 us
    all_to_all x4, waiting for transfers between devices, sum_at_owner(): lax.all_to_all(in_blocks(value, dim, devices), axis, 0, 0, tiled=True)  36.2 us
    all_gather x4, blocking collectives, from_root(): lax.all_gather(own, axis, axis=0, tiled=True)[:len(lines)]  30.9 us
    dot_general x6, matrix products, transposed(): lax.dot_general(left, right_hand, (((0,), (0,)), ((), ())), preferred_ele...  25.5 us
    all_to_all x4, waiting for transfers between devices, copy_for_each(): return lax.all_to_all(copies, axis, split_axis=0, concat_axis=0, tiled=True)  24.7 us
    all_to_all x2, starting transfers between devices, prepare(): lax.all_to_all(target, TOK, split_axis=1, concat_axis=0, tiled=True)  16.7 us
  transfers between devices with their start and end apart: 16, of which 14 were waited for; matrix products, arithmetic and copies ran while one was open for 6% of the time, Pallas kernels for 0%

commit v1 on v0

--- a/solution.py
+++ b/solution.py
@@ -103,7 +103,9 @@
         target = fetch(spans[k, 1])
         target_cols = lax.all_to_all(target, TOK, split_axis=1, concat_axis=0, tiled=True)
         sliced = lax.dynamic_slice_in_dim(source, section_index * block_width, block_width, 1)
-        source_cols = lax.all_gather(sliced, TOK, axis=0, tiled=True)
+        source_cols = jnp.concatenate(
+            lax.all_to_all(jnp.stack([sliced] * lax.axis_size(TOK)), TOK, 0, 0), axis=0
+        )
         right_side = transposed(source_cols, target_cols) * scaling
 
         def operator(direction):

time: 534 us -> 513 us (0.961)
  waiting for transfers between devices: 257 us -> 192 us
  starting transfers between devices: 47.7 us -> 67 us
  blocking collectives: 128 us -> 146 us
    all_gather x2 -> x0, waiting for transfers between devices: 142 us -> none  [prepare(): source_cols = lax.all_gather(sliced, TOK, axis=0, tiled=True)]
    all_to_all x0 -> x2, waiting for transfers between devices: none -> 64.7 us  [prepare(): lax.all_to_all(jnp.stack([sliced] * lax.axis_size(TOK)), TOK, 0, 0)]
    all_gather x4, blocking collectives: 30.9 us -> 53.6 us  [from_root(): lax.all_gather(own, axis, axis=0, tiled=True)[:len(lines)]]
    all_to_all x0 -> x2, starting transfers between devices: none -> 19 us  [prepare(): lax.all_to_all(jnp.stack([sliced] * lax.axis_size(TOK)), TOK, 0, 0)]
    all_to_all x4, waiting for transfers between devices: 36.2 us -> 42.7 us  [sum_at_owner(): lax.all_to_all(in_blocks(value, dim, devices), axis, 0, 0, tiled=True)]
  transfers between devices with their start and end apart: 16 -> 16, of which waited for: 14 -> 16; matrix products, arithmetic and copies ran while one was open for 6% -> 7% of each run, Pallas kernels for 0% -> 0%
where the time goes in v1:
time: 513 us; the launch traced here: 511 us
  waiting for transfers between devices  192 us (37%)
  blocking collectives  146 us (28%)
  starting transfers between devices  67 us (13%)
  matrix products  42.8 us (8%)
  between operations  32 us (6%)
  other arithmetic  17.1 us (3%)
  local copies, waits for them, and re-layouts  14.2 us (3%)
    psum x15, blocking collectives, over_axes(): value = lax.psum(value, axis)  92.7 us
    all_to_all x2, waiting for transfers between devices, prepare(): lax.all_to_all(jnp.stack([sliced] * lax.axis_size(TOK)), TOK, 0, 0)  64.7 us
    reduce_scatter x4, waiting for transfers between devices, from_root(): own = lax.psum_scatter(padded, axis, scatter_dimension=0, tiled=True)  53.9 us
    all_gather x4, blocking collectives, from_root(): lax.all_gather(own, axis, axis=0, tiled=True)[:len(lines)]  53.6 us
    all_to_all x4, waiting for transfers between devices, sum_at_owner(): lax.all_to_all(in_blocks(value, dim, devices), axis, 0, 0, tiled=True)  42.7 us
    dot_general x6, matrix products, transposed(): lax.dot_general(left, right_hand, (((0,), (0,)), ((), ())), preferred_ele...  25.1 us
    all_to_all x4, waiting for transfers between devices, copy_for_each(): return lax.all_to_all(copies, axis, split_axis=0, concat_axis=0, tiled=True)  24.7 us
    all_to_all x2, starting transfers between devices, prepare(): lax.all_to_all(jnp.stack([sliced] * lax.axis_size(TOK)), TOK, 0, 0)  19 us
  transfers between devices with their start and end apart: 16, of which 16 were waited for; matrix products, arithmetic and copies ran while one was open for 7% of the time, Pallas kernels for 0%

profile of v1, /device:TPU:0, one launch (start us, length us, event | category | flops | bytes accessed | tf_op | source)
XLA Modules:
  0.0 511.1 jit_solution(4433740656825645311)
XLA Ops:
  23.7 19.2 %reduce-scatter.11.cloned.1.call-done = bf16[16,4096]{1,0:T(8,128)(2,1)} async-done(((bf16[64,4096]{1,0:T(8,128)(2,1)}), bf16[16,4096]{1,0:T(8,128)(2,1)}) %reduce-scatter.11.cloned.1.call-update) | async-done | bytes 131088 | tf_op jit(solution)/shard_map/reduce_scatter | solution.py:26
  42.9 7.8 %all_gather.15 = bf16[64,4096]{1,0:T(8,128)(2,1)S(1)} all-gather(bf16[16,4096]{1,0:T(8,128)(2,1)} %reduce-scatter.11.cloned.1.call-done), channel_id=1, replica_groups=mesh['section_0'=2,'section_1'=2,'tok_0'=4,'tok_1'=4,'tok_2'=2] {'sectio..., dimensions={0}, use_global_device_ids=true | all-gather | bytes 655360 | tf_op jit(solution)/shard_map/all_gather | solution.py:27
  51.6 9.3 %all-to-all-start.3 = ((bf16[64,32,128]{2,0,1:T(8,128)(2,1)}), bf16[64,32,128]{2,0,1:T(8,128)(2,1)S(1)}, u32[]{:S(2)}, u32[]{:S(2)}) async-start(bf16[64,32,128]{2,0,1:T(8,128)(2,1)} %copy_bitcast_fusion), calls=%async_computation.7 | async-start | bytes 1048576 | tf_op jit(solution)/shard_map/all_to_all | solution.py:104
  61.0 5.6 %reduce-scatter.7.cloned.1.call-done = bf16[16,4096]{1,0:T(8,128)(2,1)} async-done(((bf16[64,4096]{1,0:T(8,128)(2,1)}), bf16[16,4096]{1,0:T(8,128)(2,1)}) %reduce-scatter.7.cloned.1.call-update) | async-done | bytes 131088 | tf_op jit(solution)/shard_map/reduce_scatter | solution.py:26
  66.6 7.5 %all_gather.13 = bf16[64,4096]{1,0:T(8,128)(2,1)S(1)} all-gather(bf16[16,4096]{1,0:T(8,128)(2,1)} %reduce-scatter.7.cloned.1.call-done), channel_id=1, replica_groups=mesh['section_0'=2,'section_1'=2,'tok_0'=4,'tok_1'=4,'tok_2'=2] {'sectio..., dimensions={0}, use_global_device_ids=true | all-gather | bytes 655360 | tf_op jit(solution)/shard_map/all_gather | solution.py:27
  76.5 7.6 %all-to-all-start.1 = ((bf16[64,32,128]{2,0,1:T(8,128)(2,1)}), bf16[64,32,128]{2,0,1:T(8,128)(2,1)S(1)}, u32[]{:S(2)}, u32[]{:S(2)}) async-start(bf16[64,32,128]{2,0,1:T(8,128)(2,1)} %copy_bitcast_fusion.1), calls=%async_computation.3 | async-start | bytes 1048576 | tf_op jit(solution)/shard_map/all_to_all | solution.py:104
  84.1 5.5 %reduce-scatter.5.cloned.1.call-done = bf16[16,4096]{1,0:T(8,128)(2,1)} async-done(((bf16[64,4096]{1,0:T(8,128)(2,1)}), bf16[16,4096]{1,0:T(8,128)(2,1)}) %reduce-scatter.5.cloned.1.call-update) | async-done | bytes 131088 | tf_op jit(solution)/shard_map/reduce_scatter | solution.py:26
  89.6 7.5 %all_gather.12 = bf16[64,4096]{1,0:T(8,128)(2,1)S(1)} all-gather(bf16[16,4096]{1,0:T(8,128)(2,1)} %reduce-scatter.5.cloned.1.call-done), channel_id=1, replica_groups=mesh['section_0'=2,'section_1'=2,'tok_0'=4,'tok_1'=4,'tok_2'=2] {'sectio..., dimensions={0}, use_global_device_ids=true | all-gather | bytes 655360 | tf_op jit(solution)/shard_map/all_gather | solution.py:27
  102.0 6.9 %all-to-all-start = ((bf16[32,64,1024]{2,1,0:T(8,128)(2,1)}), bf16[32,64,1024]{2,1,0:T(8,128)(2,1)}, u32[]{:S(2)}, u32[]{:S(2)}) async-start(bf16[32,64,1024]{2,1,0:T(8,128)(2,1)} %stack.40), calls=%async_computation.1 | async-start | bytes 8388608 | tf_op jit(solution)/shard_map/all_to_all | solution.py:107
  109.5 23.6 %reduce-scatter.9.cloned.1.call-done = bf16[16,4096]{1,0:T(8,128)(2,1)} async-done(((bf16[64,4096]{1,0:T(8,128)(2,1)}), bf16[16,4096]{1,0:T(8,128)(2,1)}) %reduce-scatter.9.cloned.1.call-update) | async-done | bytes 131088 | tf_op jit(solution)/shard_map/reduce_scatter | solution.py:26
  133.1 30.7 %all_gather.14 = bf16[64,4096]{1,0:T(8,128)(2,1)S(1)} all-gather(bf16[16,4096]{1,0:T(8,128)(2,1)} %reduce-scatter.9.cloned.1.call-done), channel_id=1, replica_groups=mesh['section_0'=2,'section_1'=2,'tok_0'=4,'tok_1'=4,'tok_2'=2] {'sectio..., dimensions={0}, use_global_device_ids=true | all-gather | bytes 655360 | tf_op jit(solution)/shard_map/all_gather | solution.py:27
  163.8 8.5 %all-to-all-done = bf16[32,64,1024]{2,1,0:T(8,128)(2,1)} async-done(((bf16[32,64,1024]{2,1,0:T(8,128)(2,1)}), bf16[32,64,1024]{2,1,0:T(8,128)(2,1)}, u32[]{:S(2)}, u32[]{:S(2)}) %all-to-all-start) | async-done | bytes 4194336 | tf_op jit(solution)/shard_map/all_to_all | solution.py:107
  174.8 12.1 %all-to-all-start.2 = ((bf16[32,64,1024]{2,1,0:T(8,128)(2,1)}), bf16[32,64,1024]{2,1,0:T(8,128)(2,1)}, u32[]{:S(2)}, u32[]{:S(2)}) async-start(bf16[32,64,1024]{2,1,0:T(8,128)(2,1)} %stack.42), calls=%async_computation.5 | async-start | bytes 8388608 | tf_op jit(solution)/shard_map/all_to_all | solution.py:107
  194.7 56.2 %all-to-all-done.2 = bf16[32,64,1024]{2,1,0:T(8,128)(2,1)} async-done(((bf16[32,64,1024]{2,1,0:T(8,128)(2,1)}), bf16[32,64,1024]{2,1,0:T(8,128)(2,1)}, u32[]{:S(2)}, u32[]{:S(2)}) %all-to-all-start.2) | async-done | bytes 4194336 | tf_op jit(solution)/shard_map/all_to_all | solution.py:107
  262.3 6.5 %all-to-all-done.4 = f32[4,512,128]{2,1,0:T(8,128)S(1)} async-done(((f32[4,512,128]{2,1,0:T(8,128)}), f32[4,512,128]{2,1,0:T(8,128)S(1)}, u32[]{:S(2)}, u32[]{:S(2)}) %all-to-all-start.4) | async-done | bytes 1048608 | tf_op jit(solution)/shard_map/all_to_all | solution.py:37
  272.4 14.3 %all-to-all-done.6 = f32[4,512,128]{2,1,0:T(8,128)S(1)} async-done(((f32[4,512,128]{2,1,0:T(8,128)}), f32[4,512,128]{2,1,0:T(8,128)S(1)}, u32[]{:S(2)}, u32[]{:S(2)}) %all-to-all-start.6) | async-done | bytes 1048608 | tf_op jit(solution)/shard_map/all_to_all | solution.py:37
  291.2 8.7 %all-to-all-done.5 = bf16[4,512,128]{2,1,0:T(8,128)(2,1)S(1)} async-done(((bf16[4,512,128]{2,1,0:T(8,128)(2,1)}), bf16[4,512,128]{2,1,0:T(8,128)(2,1)S(1)}, u32[]{:S(2)}, u32[]{:S(2)}) %all-to-all-start.5) | async-done | bytes 524320 | tf_op jit(solution)/shard_map/all_to_all | solution.py:49
  319.7 4.9 all-reduce.4
  327.0 7.8 %all-reduce.1 = (f32[2]{0:T(128)S(1)}, f32[2]{0:T(128)S(1)}) all-reduce(f32[2]{0:T(128)S(1)} %get-tuple-element.12, f32[2]{0:T(128)S(1)} %get-tuple-element.13), channel_id=1, replica_groups=mesh['section_0'=2,'section_1'=2,'tok_0'=4,'tok_1'=4,'tok_2'=2] {'tok_0'}, use_global_device_ids=true, to_apply=%region_8.9 | all-reduce | flops 4 | bytes 32 | tf_op jit(solution)/shard_map/psum | solution.py:58
  334.9 8.7 %all-reduce = (f32[2]{0:T(128)S(1)}, f32[2]{0:T(128)S(1)}) all-reduce(f32[2]{0:T(128)S(1)} %get-tuple-element.8, f32[2]{0:T(128)S(1)} %get-tuple-element.9), channel_id=1, replica_groups=mesh['section_0'=2,'section_1'=2,'tok_0'=4,'tok_1'=4,'tok_2'=2] {'tok_1'}, use_global_device_ids=true, to_apply=%region_9.10 | all-reduce | flops 4 | bytes 32 | tf_op jit(solution)/shard_map/psum | solution.py:58
  343.6 6.4 %all-reduce.2 = (f32[2]{0:T(128)S(1)}, f32[2]{0:T(128)S(1)}) all-reduce(f32[2]{0:T(128)S(1)} %get-tuple-element.6, f32[2]{0:T(128)S(1)} %get-tuple-element.7), channel_id=1, replica_groups=mesh['section_0'=2,'section_1'=2,'tok_0'=4,'tok_1'=4,'tok_2'=2] {'tok_2'}, use_global_device_ids=true, to_apply=%region_10.11 | all-reduce | flops 4 | bytes 32 | tf_op jit(solution)/shard_map/psum | solution.py:58
  363.8 9.7 %psum.152 = f32[2]{0:T(128)S(1)} all-reduce(f32[2]{0:T(128)S(1)} %psum.151), channel_id=1, replica_groups=mesh['section_0'=2,'section_1'=2,'tok_0'=4,'tok_1'=4,'tok_2'=2] {'tok_0'}, use_global_device_ids=true, to_apply=%region_24.25 | all-reduce | flops 2 | bytes 16 | tf_op jit(solution)/shard_map/psum | solution.py:58
  373.5 8.6 %psum.153 = f32[2]{0:T(128)S(1)} all-reduce(f32[2]{0:T(128)S(1)} %psum.152), channel_id=1, replica_groups=mesh['section_0'=2,'section_1'=2,'tok_0'=4,'tok_1'=4,'tok_2'=2] {'tok_1'}, use_global_device_ids=true, to_apply=%region_25.26 | all-reduce | flops 2 | bytes 16 | tf_op jit(solution)/shard_map/psum | solution.py:58
  382.2 6.4 %psum.154 = f32[2]{0:T(128)S(1)} all-reduce(f32[2]{0:T(128)S(1)} %psum.153), channel_id=1, replica_groups=mesh['section_0'=2,'section_1'=2,'tok_0'=4,'tok_1'=4,'tok_2'=2] {'tok_2'}, use_global_device_ids=true, to_apply=%region_26.27 | all-reduce | flops 2 | bytes 16 | tf_op jit(solution)/shard_map/psum | solution.py:58
  405.1 8.6 %all-to-all-done.10 = f32[4,512,128]{2,1,0:T(8,128)} async-done(((f32[4,512,128]{2,1,0:T(8,128)}), f32[4,512,128]{2,1,0:T(8,128)}, u32[]{:S(2)}, u32[]{:S(2)}) %all-to-all-start.10) | async-done | bytes 1048608 | tf_op jit(solution)/shard_map/all_to_all | solution.py:37
  419.3 13.2 %all-to-all-done.8 = f32[4,512,128]{2,1,0:T(8,128)} async-done(((f32[4,512,128]{2,1,0:T(8,128)}), f32[4,512,128]{2,1,0:T(8,128)}, u32[]{:S(2)}, u32[]{:S(2)}) %all-to-all-start.8) | async-done | bytes 1048608 | tf_op jit(solution)/shard_map/all_to_all | solution.py:37
  438.8 7.6 %all-to-all-done.11 = bf16[4,512,128]{2,1,0:T(8,128)(2,1)} async-done(((bf16[4,512,128]{2,1,0:T(8,128)(2,1)}), bf16[4,512,128]{2,1,0:T(8,128)(2,1)}, u32[]{:S(2)}, u32[]{:S(2)}) %all-to-all-start.11) | async-done | bytes 524320 | tf_op jit(solution)/shard_map/all_to_all | solution.py:49
  451.4 5.0 multiply_reduce_fusion
  460.3 5.0 multiply_reduce_fusion.1
  474.0 7.8 %psum.157 = f32[2]{0:T(128)S(1)} all-reduce(f32[2]{0:T(128)S(1)} %psum.156), channel_id=1, replica_groups=mesh['section_0'=2,'section_1'=2,'tok_0'=4,'tok_1'=4,'tok_2'=2] {'tok_0'}, use_global_device_ids=true, to_apply=%region_33.34 | all-reduce | flops 2 | bytes 16 | tf_op jit(solution)/shard_map/psum | solution.py:58
  481.8 8.7 %psum.158 = f32[2]{0:T(128)S(1)} all-reduce(f32[2]{0:T(128)S(1)} %psum.157), channel_id=1, replica_groups=mesh['section_0'=2,'section_1'=2,'tok_0'=4,'tok_1'=4,'tok_2'=2] {'tok_1'}, use_global_device_ids=true, to_apply=%region_34.35 | all-reduce | flops 2 | bytes 16 | tf_op jit(solution)/shard_map/psum | solution.py:58
  490.5 6.4 %psum.159 = f32[2]{0:T(128)S(1)} all-reduce(f32[2]{0:T(128)S(1)} %psum.158), channel_id=1, replica_groups=mesh['section_0'=2,'section_1'=2,'tok_0'=4,'tok_1'=4,'tok_2'=2] {'tok_2'}, use_global_device_ids=true, to_apply=%region_35.36 | all-reduce | flops 2 | bytes 16 | tf_op jit(solution)/shard_map/psum | solution.py:58
  (64 shorter events, 126.4 us)
Async XLA Ops:
  7.2 35.7 %reduce-scatter.11.cloned.1.call-start = ((), (), s32[]{:S(2)}) async-start(), calls=%async_computation.19 | async-start | bytes 655360 | tf_op jit(solution)/shard_map/reduce_scatter | solution.py:26
  22.2 44.4 %reduce-scatter.7.cloned.1.call-start = ((), (), s32[]{:S(2)}) async-start(), calls=%async_computation.17 | async-start | bytes 655360 | tf_op jit(solution)/shard_map/reduce_scatter | solution.py:26
  22.9 66.7 %reduce-scatter.5.cloned.1.call-start = ((), (), s32[]{:S(2)}) async-start(), calls=%async_computation.16 | async-start | bytes 655360 | tf_op jit(solution)/shard_map/reduce_scatter | solution.py:26
  51.6 24.8 %all-to-all-start.3 = ((bf16[64,32,128]{2,0,1:T(8,128)(2,1)}), bf16[64,32,128]{2,0,1:T(8,128)(2,1)S(1)}, u32[]{:S(2)}, u32[]{:S(2)}) async-start(bf16[64,32,128]{2,0,1:T(8,128)(2,1)} %copy_bitcast_fusion), calls=%async_computation.7 | async-start | bytes 1048576 | tf_op jit(solution)/shard_map/all_to_all | solution.py:104
  76.5 23.1 %all-to-all-start.1 = ((bf16[64,32,128]{2,0,1:T(8,128)(2,1)}), bf16[64,32,128]{2,0,1:T(8,128)(2,1)S(1)}, u32[]{:S(2)}, u32[]{:S(2)}) async-start(bf16[64,32,128]{2,0,1:T(8,128)(2,1)} %copy_bitcast_fusion.1), calls=%async_computation.3 | async-start | bytes 1048576 | tf_op jit(solution)/shard_map/all_to_all | solution.py:104
  102.0 70.2 %all-to-all-start = ((bf16[32,64,1024]{2,1,0:T(8,128)(2,1)}), bf16[32,64,1024]{2,1,0:T(8,128)(2,1)}, u32[]{:S(2)}, u32[]{:S(2)}) async-start(bf16[32,64,1024]{2,1,0:T(8,128)(2,1)} %stack.40), calls=%async_computation.1 | async-start | bytes 8388608 | tf_op jit(solution)/shard_map/all_to_all | solution.py:107
  108.9 24.2 %reduce-scatter.9.cloned.1.call-start = ((), (), s32[]{:S(2)}) async-start(), calls=%async_computation.18 | async-start | bytes 655360 | tf_op jit(solution)/shard_map/reduce_scatter | solution.py:26
  174.8 76.2 %all-to-all-start.2 = ((bf16[32,64,1024]{2,1,0:T(8,128)(2,1)}), bf16[32,64,1024]{2,1,0:T(8,128)(2,1)}, u32[]{:S(2)}, u32[]{:S(2)}) async-start(bf16[32,64,1024]{2,1,0:T(8,128)(2,1)} %stack.42), calls=%async_computation.5 | async-start | bytes 8388608 | tf_op jit(solution)/shard_map/all_to_all | solution.py:107
  250.9 17.9 %all-to-all-start.4 = ((f32[4,512,128]{2,1,0:T(8,128)}), f32[4,512,128]{2,1,0:T(8,128)S(1)}, u32[]{:S(2)}, u32[]{:S(2)}) async-start(f32[4,512,128]{2,1,0:T(8,128)} %fusion.7), calls=%async_computation.8 | async-start | bytes 2097152 | tf_op jit(solution)/shard_map/all_to_all | solution.py:37
  268.9 17.9 %all-to-all-start.6 = ((f32[4,512,128]{2,1,0:T(8,128)}), f32[4,512,128]{2,1,0:T(8,128)S(1)}, u32[]{:S(2)}, u32[]{:S(2)}) async-start(f32[4,512,128]{2,1,0:T(8,128)} %fusion.10), calls=%async_computation.10 | async-start | bytes 2097152 | tf_op jit(solution)/shard_map/all_to_all | solution.py:37
  287.6 12.3 %all-to-all-start.5 = ((bf16[4,512,128]{2,1,0:T(8,128)(2,1)}), bf16[4,512,128]{2,1,0:T(8,128)(2,1)S(1)}, u32[]{:S(2)}, u32[]{:S(2)}) async-start(bf16[4,512,128]{2,1,0:T(8,128)(2,1)} %broadcast_in_dim.12), calls=%async_computation.9 | async-start | bytes 1048576 | tf_op jit(solution)/shard_map/all_to_all | solution.py:49
  300.8 12.3 %all-to-all-start.7 = ((bf16[4,512,128]{2,1,0:T(8,128)(2,1)}), bf16[4,512,128]{2,1,0:T(8,128)(2,1)S(1)}, u32[]{:S(2)}, u32[]{:S(2)}) async-start(bf16[4,512,128]{2,1,0:T(8,128)(2,1)} %broadcast_in_dim.13), calls=%async_computation.11 | async-start | bytes 1048576 | tf_op jit(solution)/shard_map/all_to_all | solution.py:49
  395.0 18.7 %all-to-all-start.10 = ((f32[4,512,128]{2,1,0:T(8,128)}), f32[4,512,128]{2,1,0:T(8,128)}, u32[]{:S(2)}, u32[]{:S(2)}) async-start(f32[4,512,128]{2,1,0:T(8,128)} %fusion.12), calls=%async_computation.14 | async-start | bytes 2097152 | tf_op jit(solution)/shard_map/all_to_all | solution.py:37
  413.7 18.8 %all-to-all-start.8 = ((f32[4,512,128]{2,1,0:T(8,128)}), f32[4,512,128]{2,1,0:T(8,128)}, u32[]{:S(2)}, u32[]{:S(2)}) async-start(f32[4,512,128]{2,1,0:T(8,128)} %fusion.14), calls=%async_computation.12 | async-start | bytes 2097152 | tf_op jit(solution)/shard_map/all_to_all | solution.py:37
  433.4 13.0 %all-to-all-start.11 = ((bf16[4,512,128]{2,1,0:T(8,128)(2,1)}), bf16[4,512,128]{2,1,0:T(8,128)(2,1)}, u32[]{:S(2)}, u32[]{:S(2)}) async-start(bf16[4,512,128]{2,1,0:T(8,128)(2,1)} %broadcast_in_dim.15), calls=%async_computation.15 | async-start | bytes 1048576 | tf_op jit(solution)/shard_map/all_to_all | solution.py:49
  447.2 13.0 %all-to-all-start.9 = ((bf16[4,512,128]{2,1,0:T(8,128)(2,1)}), bf16[4,512,128]{2,1,0:T(8,128)(2,1)}, u32[]{:S(2)}, u32[]{:S(2)}) async-start(bf16[4,512,128]{2,1,0:T(8,128)(2,1)} %broadcast_in_dim.14), calls=%async_computation.13 | async-start | bytes 1048576 | tf_op jit(solution)/shard_map/all_to_all | solution.py:49
Sparse Core Ops, SparseCore 0:
  22.3 20.5 reduce-scatter.10
  45.8 20.6 reduce-scatter.6
  69.5 20.0 reduce-scatter.4
  111.8 21.2 reduce-scatter.8
